TPU v7x, 32 devices: a whole 2x2x4 slice. The times are simulated.
32 devices in a mesh: dp: 2 (over x), tp: 16 (over z, y, core).
Axes of the slice: x: 2, y: 2, z: 4, core: 2. Of those that a mesh axis runs over, the one named last changes fastest.
Arguments:
- hidden: bfloat16 [32, 12, 2560], P('dp'), parts along dimension 0
- norm_w: bfloat16 [2560], replicated
- embedding: bfloat16 [262144, 2560], P('tp')
- draft_ids: int32 [32, 12], P('dp'), parts along dimension 0
Outputs:
- output 1: float32 [32, 12], P('dp'), parts along dimension 0
- output 2: float32 [32, 12], P('dp'), parts along dimension 0
There are 2 independent parts. A program takes and returns all parts, laid end to end along the dimension named above; an argument that names none is the same for every part.
All inputs are finite; a program needn't handle non-finite values.
Results may differ from a plain program's by a relative error of at most 0.001.
Values sent between devices are 32-bit elements.
A program may use at most 1 GiB of HBM per device.

v0:
```python
import jax
import jax.numpy as jnp
from jax import lax
from jax.sharding import PartitionSpec as P, NamedSharding

EPS = 1e-6


def solution(mesh):
    def local_part(hidden, norm_w, embedding, draft_ids):
        shard_rows = embedding.shape[0]
        offset = lax.axis_index("tp") * shard_rows
        x_float = hidden.astype(jnp.float32)
        mean_sq = jnp.mean(x_float * x_float, axis=-1, keepdims=True)
        normed = (x_float * lax.rsqrt(mean_sq + EPS) * (1.0 + norm_w.astype(jnp.float32))).astype(jnp.bfloat16)
        logits = jnp.einsum("bgd,vd->bgv", normed, embedding, preferred_element_type=jnp.float32)
        local_max = jnp.max(logits, axis=-1)
        row_max = lax.pmax(local_max, "tp")
        exp_shift = jnp.exp(logits - row_max[..., None])
        exp_total = lax.psum(jnp.sum(exp_shift, axis=-1), "tp")
        weighted = lax.psum(jnp.sum(exp_shift * logits, axis=-1), "tp")
        local_ids = draft_ids - offset
        is_owned = (local_ids >= 0) & (local_ids < shard_rows)
        safe_ids = jnp.clip(local_ids, 0, shard_rows - 1)
        local_pick = jnp.take_along_axis(logits, safe_ids[..., None], axis=-1)[..., 0]
        picked = lax.psum(jnp.where(is_owned, local_pick, 0.0), "tp")
        log_norm = row_max + jnp.log(exp_total)
        return picked - log_norm, log_norm - weighted / exp_total

    return jax.shard_map(local_part, mesh=mesh, in_specs=(P("dp", None, None), P(None), P("tp", None), P("dp", None)), out_specs=(P("dp", None), P("dp", None)), check_vma=False)
```

profile of v0, /device:TPU:0, one launch (start us, length us, event | category | flops | bytes accessed | tf_op | source)
XLA Modules:
  0.0 147.2 jit_solution(11050392704676170559)
XLA Ops:
  0.6 0.8 copy.12
  1.4 1.5 fusion.3
  3.0 0.1 copy.13
  3.0 0.1 reshape.39
  3.1 0.7 convert_add_fusion
  3.8 38.4 %fusion.16 = (f32[16,12]{0,1:T(8,128)S(1)}, f32[16,12,16384]{2,0,1:T(8,128)}) fusion(bf16[16384,2560]{1,0:T(8,128)(2,1)} %param.6, bf16[16,12,2560]{2,0,1:T(8,128)(2,1)} %param.4, f32[2560]{0:T(1024)S(1)} %convert_add_fusion, f32[16,12]{0,1:T(8,128)S(1)} %add_rsqrt_fusion), kind=kOutput, calls=%fused_computation.30 | convolution fusion | flops 16111239168 | bytes 97463808 | tf_op jit(solution)/shard_map/bgd,vd->bgv/dot_general | solution.py:16
  42.2 35.5 %pmax.7 = f32[16,12]{0,1:T(8,128)S(1)} all-reduce(f32[16,12]{0,1:T(8,128)S(1)} %get-tuple-element.13), channel_id=1, replica_groups=mesh['dp'=2,'tp'=16] {'tp'}, use_global_device_ids=true, to_apply=%region_3.0 | all-reduce | flops 192 | bytes 1536 | tf_op jit(solution)/shard_map/pmax | solution.py:18
  77.7 3.1 %gather_fusion = f32[192]{0:T(256)S(1)} fusion(f32[16,12,16384]{2,0,1:T(8,128)} %get-tuple-element.14, s32[192]{0:T(256)S(1)} %reshape.39), kind=kCustom, calls=%fused_computation | custom fusion | bytes 3840 | tf_op jit(solution)/shard_map/jit(take_along_axis)/gather | solution.py:25
  80.7 7.3 %multiply_reduce_fusion = (f32[16,12]{0,1:T(8,128)S(1)}, f32[16,12]{0,1:T(8,128)S(1)}) fusion(f32[16,12,16384]{2,0,1:T(8,128)} %get-tuple-element.14, f32[16,12]{0,1:T(8,128)S(1)} %pmax.7), kind=kLoop, calls=%fused_computation.3 | loop fusion | flops 12582528 | bytes 12585216 | tf_op jit(solution)/shard_map/reduce_sum | solution.py:21
  88.0 0.1 gather.7
  88.1 0.1 copy.14
  88.2 57.6 %all-reduce = (f32[16,12]{0,1:T(8,128)S(1)}, f32[16,12]{0,1:T(8,128)S(1)}, f32[16,12]{0,1:T(8,128)S(1)}) all-reduce(f32[16,12]{0,1:T(8,128)S(1)} %select_select_fusion, f32[16,12]{0,1:T(8,128)S(1)} %get-tuple-element.7, f32[16,12]{0,1:T(8,128)S(1)} %get-tuple-element.6), channel_id=1, replica_groups=mesh['dp'=2,'tp'=16] {'tp'}, use_global_device_ids=true, to_apply=%region_1.0 | all-reduce | flops 576 | bytes 4608 | tf_op jit(solution)/shard_map/psum | solution.py:26
  145.9 0.7 copy.16
  146.5 0.7 copy.15
  (8 shorter events, 0.1 us)
where the time goes:
time: 148 us; the launch traced here: 147 us
  blocking collectives  93.1 us (63%)
  matrix products  38.4 us (26%)
  other arithmetic  9.51 us (6%)
  local copies, waits for them, and re-layouts  5.53 us (4%)
    psum x1, blocking collectives, local_part(): picked = lax.psum(jnp.where(is_owned, local_pick, 0.0), 'tp')  57.6 us
    dot_general x1, matrix products, local_part(): jnp.einsum('bgd,vd->bgv', normed, embedding, preferred_element_type=jnp.f...  38.4 us
    pmax x1, blocking collectives, local_part(): row_max = lax.pmax(local_max, 'tp')  35.5 us
    reduce_sum x1, other arithmetic, local_part(): weighted = lax.psum(jnp.sum(exp_shift * logits, axis=-1), 'tp')  7.3 us
    gather x5, local copies, waits for them, and re-layouts, local_part(): jnp.take_along_axis(logits, safe_ids[..., None], axis=-1)[..., 0]  3.38 us

commit v1 on v0

v1 whole, which is shorter than its diff:
```python
import functools

import jax
import jax.numpy as jnp
from jax import lax
from jax.experimental import pallas as pl
from jax.experimental.pallas import tpu as pltpu
from jax.sharding import PartitionSpec as P

EPS = 1e-6
LANES = 128
CHUNK = 512
SLOTS = 14
MESH = pl.DeviceIdType.MESH


def head_kernel(tp, x_hbm, w_ref, e_hbm, ids_ref, out_ref, x_buf, h_buf, e_buf, z_a, z_b,
                idp, m_ref, s_ref, a_ref, p_ref, stats, recv, x_sem, e_sem, send_sem, recv_sem):
    groups, batch, depth = x_hbm.shape
    tokens = groups * batch
    rows = e_hbm.shape[0]
    steps = rows // CHUNK
    width = h_buf.shape[0]
    me = lax.axis_index("tp")

    barrier = pltpu.get_barrier_semaphore()
    x_copy = pltpu.make_async_copy(x_hbm, x_buf, x_sem)
    x_copy.start()

    def e_copy(step, slot):
        first = pl.multiple_of(step * CHUNK, CHUNK)
        return pltpu.make_async_copy(e_hbm.at[pl.ds(first, CHUNK)], e_buf.at[slot], e_sem.at[slot])

    for slot in range(SLOTS):
        e_copy(slot, slot).start()
    for k in range(1, tp):
        pl.semaphore_signal(barrier, inc=1, device_id={"tp": lax.rem(me + k, tp)}, device_id_type=MESH)

    idp[...] = jnp.full_like(idp, -1)
    idp[0:batch, 0:groups] = ids_ref[...]
    by_group = jnp.transpose(idp[...])
    sub = lax.broadcasted_iota(jnp.int32, (8, LANES), 0)
    lane = lax.broadcasted_iota(jnp.int32, (8, LANES), 1)
    id_rows = []
    for half in range(width // LANES):
        part = pltpu.roll(by_group[8 * half:8 * half + 8], 0, 1, stride=batch, stride_axis=0)
        part = jnp.where(lane // batch == sub, part, 0)
        id_rows.append(jnp.sum(part, axis=0, keepdims=True))
    id_row = jnp.concatenate(id_rows, axis=1)
    sub_w = lax.broadcasted_iota(jnp.int32, (8, width), 0)
    lane_w = lax.broadcasted_iota(jnp.int32, (8, width), 1)
    wanted = jnp.where(lane_w < tokens, id_row - me * rows - sub_w, -(1 << 30))

    m_ref[...] = jnp.full_like(m_ref, -jnp.inf)
    s_ref[...] = jnp.zeros_like(s_ref)
    a_ref[...] = jnp.zeros_like(a_ref)
    p_ref[...] = jnp.zeros_like(p_ref)

    h_buf[tokens:width, :] = jnp.zeros((width - tokens, depth), h_buf.dtype)
    gain = 1.0 + w_ref[...].astype(jnp.float32)
    x_copy.wait()

    def norm(g, _):
        x = x_buf[g].astype(jnp.float32)
        mean_sq = jnp.sum(x * x, axis=-1, keepdims=True) * (1.0 / depth)
        normed = x * lax.rsqrt(mean_sq + EPS) * gain
        h_buf[pl.ds(pl.multiple_of(g * batch, batch), batch), :] = normed.astype(h_buf.dtype)
        return _

    lax.fori_loop(0, groups, norm, 0)

    def logits(slot):
        return lax.dot_general(e_buf[slot], h_buf[...], (((1,), (1,)), ((), ())),
                               preferred_element_type=jnp.float32)

    def fold(z_ref, step):
        z = z_ref[...].reshape(CHUNK // 8, 8, width)
        m_old = m_ref[...]
        m_new = jnp.maximum(m_old, jnp.max(z, axis=0))
        scale = jnp.exp(m_old - m_new)
        e = jnp.exp(z - m_new[None])
        m_ref[...] = m_new
        s_ref[...] = s_ref[...] * scale + jnp.sum(e, axis=0)
        a_ref[...] = a_ref[...] * scale + jnp.sum(e * z, axis=0)
        here = wanted - step * CHUNK
        at = 8 * lax.broadcasted_iota(jnp.int32, z.shape, 0)
        p_ref[...] += jnp.sum(jnp.where(here[None] == at, z, 0.0), axis=0)

    def one(step, into, other):
        slot = lax.rem(step, SLOTS)
        e_copy(step, slot).wait()
        into[...] = logits(slot)
        if other is not None:
            fold(other, step - 1)

        @pl.when(step + SLOTS < steps)
        def _():
            e_copy(step + SLOTS, slot).start()

    one(0, z_a, None)

    def pair(i, _):
        one(2 * i + 1, z_b, z_a)
        one(2 * i + 2, z_a, z_b)
        return _

    lax.fori_loop(0, (steps - 2) // 2, pair, 0)
    one(steps - 1, z_b, z_a)
    fold(z_b, steps - 1)

    m8 = m_ref[...]
    m1 = jnp.max(m8, axis=0, keepdims=True)
    c8 = jnp.exp(m8 - m1)
    s1 = jnp.sum(c8 * s_ref[...], axis=0, keepdims=True)
    a1 = jnp.sum(c8 * a_ref[...], axis=0, keepdims=True)
    p1 = jnp.sum(p_ref[...], axis=0, keepdims=True)
    own = jnp.concatenate([m1, s1, a1, p1], axis=0)
    stats[...] = own
    recv[me] = own

    pl.semaphore_wait(barrier, tp - 1)

    def send(k):
        peer = lax.rem(me + k, tp)
        return pltpu.make_async_remote_copy(
            src_ref=stats, dst_ref=recv.at[me], send_sem=send_sem.at[k], recv_sem=recv_sem.at[k],
            device_id={"tp": peer}, device_id_type=MESH)

    for k in range(1, tp):
        send(k).start()
    for k in range(1, tp):
        send(k).wait()

    r = recv[...]
    m = r[:, 0, :]
    top = jnp.max(m, axis=0, keepdims=True)
    c = jnp.exp(m - top)
    total = jnp.sum(c * r[:, 1, :], axis=0, keepdims=True)
    weighted = jnp.sum(c * r[:, 2, :], axis=0, keepdims=True)
    picked = jnp.sum(r[:, 3, :], axis=0, keepdims=True)
    log_norm = top + jnp.log(total)
    log_prob = picked - log_norm
    entropy = log_norm - weighted / total

    out = jnp.zeros((batch, LANES), jnp.float32)
    out_lane = lax.broadcasted_iota(jnp.int32, (batch, LANES), 1)
    row = lax.broadcasted_iota(jnp.int32, (LANES, LANES), 0)
    for half in range(width // LANES):
        cut = slice(half * LANES, (half + 1) * LANES)
        both = jnp.where(row < LANES // 2, log_prob[:, cut], entropy[:, cut])
        col = jnp.transpose(both)
        for j in range(LANES // batch):
            g = half * (LANES // batch) + j
            if g < groups:
                mine = (out_lane == g) | (out_lane == g + LANES // 2)
                out = jnp.where(mine, col[j * batch:(j + 1) * batch], out)
    out_ref[0] = out[:, 0:groups]
    out_ref[1] = out[:, LANES // 2:LANES // 2 + groups]


def solution(mesh):
    tp = mesh.shape["tp"]

    def local_part(hidden, norm_w, embedding, draft_ids):
        batch, groups, depth = hidden.shape
        width = pl.cdiv(batch * groups, 2 * LANES) * 2 * LANES
        x = jnp.transpose(hidden, (1, 0, 2))
        any_space = pl.BlockSpec(memory_space=pl.ANY)
        vmem = pl.BlockSpec(memory_space=pltpu.VMEM)
        out = pl.pallas_call(
            functools.partial(head_kernel, tp),
            out_shape=jax.ShapeDtypeStruct((2, batch, groups), jnp.float32),
            in_specs=[any_space, vmem, any_space, vmem],
            out_specs=vmem,
            scratch_shapes=[
                pltpu.VMEM((groups, batch, depth), hidden.dtype),
                pltpu.VMEM((width, depth), jnp.bfloat16),
                pltpu.VMEM((SLOTS, CHUNK, depth), embedding.dtype),
                pltpu.VMEM((CHUNK, width), jnp.float32),
                pltpu.VMEM((CHUNK, width), jnp.float32),
                pltpu.VMEM((LANES, LANES), jnp.int32),
                pltpu.VMEM((8, width), jnp.float32),
                pltpu.VMEM((8, width), jnp.float32),
                pltpu.VMEM((8, width), jnp.float32),
                pltpu.VMEM((8, width), jnp.float32),
                pltpu.VMEM((4, width), jnp.float32),
                pltpu.VMEM((tp, 4, width), jnp.float32),
                pltpu.SemaphoreType.DMA,
                pltpu.SemaphoreType.DMA((SLOTS,)),
                pltpu.SemaphoreType.DMA((tp,)),
                pltpu.SemaphoreType.DMA((tp,)),
            ],
            compiler_params=pltpu.CompilerParams(
                collective_id=0, has_side_effects=True, vmem_limit_bytes=60 * 1024 * 1024),
        )(x, norm_w.reshape(1, depth), embedding, draft_ids)
        return out[0], out[1]

    return jax.shard_map(
        local_part, mesh=mesh,
        in_specs=(P("dp", None, None), P(None), P("tp", None), P("dp", None)),
        out_specs=(P("dp", None), P("dp", None)), check_vma=False)
```

time: 148 us -> 74.5 us (0.50)
  blocking collectives: 93.1 us -> 0 us
  Pallas kernels: 0 us -> 70.8 us
  matrix products: 38.4 us -> 0 us
  other arithmetic: 9.51 us -> 0 us
  local copies, waits for them, and re-layouts: 5.53 us -> 2.62 us
    pallas_call x0 -> x1, Pallas kernels: none -> 70.8 us  [local_part(): pl.pallas_call(functools.partial(head_kernel, tp), out_shape=jax.ShapeDty...]
    psum x1 -> x0, blocking collectives: 57.6 us -> none  [local_part(): picked = lax.psum(jnp.where(is_owned, local_pick, 0.0), 'tp')]
    dot_general x1 -> x0, matrix products: 38.4 us -> none  [local_part(): jnp.einsum('bgd,vd->bgv', normed, embedding, preferred_element_type=jnp.f...]
    pmax x1 -> x0, blocking collectives: 35.5 us -> none  [local_part(): row_max = lax.pmax(local_max, 'tp')]
    reduce_sum x2 -> x0, other arithmetic: 8.76 us -> none  [the longest x1 7.3 us: local_part(): weighted = lax.psum(jnp.sum(exp_shift * logits, axis=-1), 'tp')]
    gather x5 -> x0, local copies, waits for them, and re-layouts: 3.38 us -> none  [local_part(): jnp.take_along_axis(logits, safe_ids[..., None], axis=-1)[..., 0]]
    unnamed x5 -> x0, local copies, waits for them, and re-layouts: 2.15 us -> none
where the time goes in v1:
time: 74.5 us; the launch traced here: 74.1 us
  Pallas kernels  70.8 us (95%)
  local copies, waits for them, and re-layouts  2.62 us (4%)
    pallas_call x1, Pallas kernels, local_part(): pl.pallas_call(functools.partial(head_kernel, tp), out_shape=jax.ShapeDty...  70.8 us

profile of v1, /device:TPU:0, one launch (start us, length us, event | category | flops | bytes accessed | tf_op | source)
XLA Modules:
  0.0 74.1 jit_solution(16601670424753366250)
XLA Ops:
  0.6 1.3 %reshape.7.w_ref = bf16[1,2560]{1,0:T(2,128)(2,1)} reshape(bf16[2560]{0:T(1024)(128)(2,1)} %param.5) | data formatting | bytes 10240 | tf_op jit(solution)/shard_map/reshape | solution.py:195
  1.9 70.8 %shard_map.59 = f32[2,16,12]{2,1,0:T(8,128)} custom-call(bf16[12,16,2560]{2,1,0:T(8,128)(2,1)} %bitcast.5, bf16[1,2560]{1,0:T(2,128)(2,1)} %reshape.7.w_ref, bf16[16384,2560]{1,0:T(8,128)(2,1)} %e_hbm.1, s32[16,12]{1,0:T(8,128)} %ids_ref.1), custom_call_target="tpu_custom_call" | custom-call | tf_op jit(solution)/shard_map/pallas_call | solution.py:170
  72.7 1.3 %slice_bitcast_fusion = (f32[16,12]{1,0:T(8,128)}, f32[16,12]{1,0:T(8,128)}) fusion(f32[2,16,12]{2,1,0:T(8,128)} %shard_map.59), kind=kLoop, calls=%fused_computation | loop fusion | bytes 3072 | tf_op jit(solution)/shard_map/squeeze | solution.py:196

commit v2 on v1

--- a/solution.py
+++ b/solution.py
@@ -10,7 +10,7 @@
 EPS = 1e-6
 LANES = 128
 CHUNK = 512
-SLOTS = 14
+SLOTS = 4
 MESH = pl.DeviceIdType.MESH
 
 

time: 74.5 us -> 66.9 us (0.90)
  Pallas kernels: 70.8 us -> 63.2 us
    pallas_call x1, Pallas kernels: 70.8 us -> 63.2 us  [local_part(): pl.pallas_call(functools.partial(head_kernel, tp), out_shape=jax.ShapeDty...]
where the time goes in v2:
time: 66.9 us; the launch traced here: 66.5 us
  Pallas kernels  63.2 us (94%)
  local copies, waits for them, and re-layouts  2.62 us (4%)
    pallas_call x1, Pallas kernels, local_part(): pl.pallas_call(functools.partial(head_kernel, tp), out_shape=jax.ShapeDty...  63.2 us

profile of v2, /device:TPU:0, one launch (start us, length us, event | category | flops | bytes accessed | tf_op | source)
XLA Modules:
  0.0 66.5 jit_solution(3374182673077501556)
XLA Ops:
  0.6 1.3 %reshape.7.w_ref = bf16[1,2560]{1,0:T(2,128)(2,1)} reshape(bf16[2560]{0:T(1024)(128)(2,1)} %param.5) | data formatting | bytes 10240 | tf_op jit(solution)/shard_map/reshape | solution.py:195
  1.9 63.2 %shard_map.59 = f32[2,16,12]{2,1,0:T(8,128)} custom-call(bf16[12,16,2560]{2,1,0:T(8,128)(2,1)} %bitcast.5, bf16[1,2560]{1,0:T(2,128)(2,1)} %reshape.7.w_ref, bf16[16384,2560]{1,0:T(8,128)(2,1)} %e_hbm.1, s32[16,12]{1,0:T(8,128)} %ids_ref.1), custom_call_target="tpu_custom_call" | custom-call | tf_op jit(solution)/shard_map/pallas_call | solution.py:170
  65.2 1.3 %slice_bitcast_fusion = (f32[16,12]{1,0:T(8,128)}, f32[16,12]{1,0:T(8,128)}) fusion(f32[2,16,12]{2,1,0:T(8,128)} %shard_map.59), kind=kLoop, calls=%fused_computation | loop fusion | bytes 3072 | tf_op jit(solution)/shard_map/squeeze | solution.py:196

commit v3 on v2

--- a/solution.py
+++ b/solution.py
@@ -9,8 +9,9 @@
 
 EPS = 1e-6
 LANES = 128
-CHUNK = 512
-SLOTS = 4
+BLOCK = 512
+CHUNK = 2 * BLOCK
+SLOTS = 7
 MESH = pl.DeviceIdType.MESH
 
 
@@ -31,8 +32,11 @@
         first = pl.multiple_of(step * CHUNK, CHUNK)
         return pltpu.make_async_copy(e_hbm.at[pl.ds(first, CHUNK)], e_buf.at[slot], e_sem.at[slot])
 
-    for slot in range(SLOTS):
+    def fill(slot, c):
         e_copy(slot, slot).start()
+        return c
+
+    lax.fori_loop(0, SLOTS, fill, 0)
     for k in range(1, tp):
         pl.semaphore_signal(barrier, inc=1, device_id={"tp": lax.rem(me + k, tp)}, device_id_type=MESH)
 
@@ -69,12 +73,12 @@
 
     lax.fori_loop(0, groups, norm, 0)
 
-    def logits(slot):
-        return lax.dot_general(e_buf[slot], h_buf[...], (((1,), (1,)), ((), ())),
+    def logits(slot, part):
+        return lax.dot_general(e_buf[slot, pl.ds(part * BLOCK, BLOCK)], h_buf[...], (((1,), (1,)), ((), ())),
                                preferred_element_type=jnp.float32)
 
-    def fold(z_ref, step):
-        z = z_ref[...].reshape(CHUNK // 8, 8, width)
+    def fold(z_ref, first):
+        z = z_ref[...].reshape(BLOCK // 8, 8, width)
         m_old = m_ref[...]
         m_new = jnp.maximum(m_old, jnp.max(z, axis=0))
         scale = jnp.exp(m_old - m_new)
@@ -82,31 +86,33 @@
         m_ref[...] = m_new
         s_ref[...] = s_ref[...] * scale + jnp.sum(e, axis=0)
         a_ref[...] = a_ref[...] * scale + jnp.sum(e * z, axis=0)
-        here = wanted - step * CHUNK
+        here = wanted - first
         at = 8 * lax.broadcasted_iota(jnp.int32, z.shape, 0)
         p_ref[...] += jnp.sum(jnp.where(here[None] == at, z, 0.0), axis=0)
 
-    def one(step, into, other):
-        slot = lax.rem(step, SLOTS)
-        e_copy(step, slot).wait()
-        into[...] = logits(slot)
-        if other is not None:
-            fold(other, step - 1)
-
-        @pl.when(step + SLOTS < steps)
+    e_copy(0, 0).wait()
+    z_a[...] = logits(0, 0)
+
+    def chunk(i, c):
+        slot = lax.rem(i, SLOTS)
+        z_b[...] = logits(slot, 1)
+        fold(z_a, i * CHUNK)
+
+        @pl.when(i + SLOTS < steps)
         def _():
-            e_copy(step + SLOTS, slot).start()
-
-    one(0, z_a, None)
-
-    def pair(i, _):
-        one(2 * i + 1, z_b, z_a)
-        one(2 * i + 2, z_a, z_b)
-        return _
-
-    lax.fori_loop(0, (steps - 2) // 2, pair, 0)
-    one(steps - 1, z_b, z_a)
-    fold(z_b, steps - 1)
+            e_copy(i + SLOTS, slot).start()
+
+        after = lax.rem(i + 1, SLOTS)
+        e_copy(i + 1, after).wait()
+        z_a[...] = logits(after, 0)
+        fold(z_b, i * CHUNK + BLOCK)
+        return c
+
+    lax.fori_loop(0, steps - 1, chunk, 0)
+    last = (steps - 1) * CHUNK
+    z_b[...] = logits((steps - 1) % SLOTS, 1)
+    fold(z_a, last)
+    fold(z_b, last + BLOCK)
 
     m8 = m_ref[...]
     m1 = jnp.max(m8, axis=0, keepdims=True)
@@ -176,8 +182,8 @@
                 pltpu.VMEM((groups, batch, depth), hidden.dtype),
                 pltpu.VMEM((width, depth), jnp.bfloat16),
                 pltpu.VMEM((SLOTS, CHUNK, depth), embedding.dtype),
-                pltpu.VMEM((CHUNK, width), jnp.float32),
-                pltpu.VMEM((CHUNK, width), jnp.float32),
+                pltpu.VMEM((BLOCK, width), jnp.float32),
+                pltpu.VMEM((BLOCK, width), jnp.float32),
                 pltpu.VMEM((LANES, LANES), jnp.int32),
                 pltpu.VMEM((8, width), jnp.float32),
                 pltpu.VMEM((8, width), jnp.float32),

time: 66.9 us -> 64.5 us (0.964)
  Pallas kernels: 63.2 us -> 60.8 us
    pallas_call x1, Pallas kernels: 63.2 us -> 60.8 us  [local_part(): pl.pallas_call(functools.partial(head_kernel, tp), out_shape=jax.ShapeDty...]
where the time goes in v3:
time: 64.5 us; the launch traced here: 64.1 us
  Pallas kernels  60.8 us (94%)
  local copies, waits for them, and re-layouts  2.62 us (4%)
    pallas_call x1, Pallas kernels, local_part(): pl.pallas_call(functools.partial(head_kernel, tp), out_shape=jax.ShapeDty...  60.8 us
    squeeze x1, local copies, waits for them, and re-layouts, local_part(): return (out[0], out[1])  1.32 us
    reshape x1, local copies, waits for them, and re-layouts, local_part(): norm_w.reshape(1, depth)  1.3 us

profile of v3, /device:TPU:0, one launch (start us, length us, event | category | flops | bytes accessed | tf_op | source)
XLA Modules:
  0.0 64.1 jit_solution(17742020254670438379)
XLA Ops:
  0.6 1.3 %reshape.7.w_ref = bf16[1,2560]{1,0:T(2,128)(2,1)} reshape(bf16[2560]{0:T(1024)(128)(2,1)} %param.5) | data formatting | bytes 10240 | tf_op jit(solution)/shard_map/reshape | solution.py:201
  1.9 60.8 %shard_map.59 = f32[2,16,12]{2,1,0:T(8,128)} custom-call(bf16[12,16,2560]{2,1,0:T(8,128)(2,1)} %bitcast.5, bf16[1,2560]{1,0:T(2,128)(2,1)} %reshape.7.w_ref, bf16[16384,2560]{1,0:T(8,128)(2,1)} %e_hbm.1, s32[16,12]{1,0:T(8,128)} %ids_ref.1), custom_call_target="tpu_custom_call" | custom-call | tf_op jit(solution)/shard_map/pallas_call | solution.py:176
  62.8 1.3 %slice_bitcast_fusion = (f32[16,12]{1,0:T(8,128)}, f32[16,12]{1,0:T(8,128)}) fusion(f32[2,16,12]{2,1,0:T(8,128)} %shard_map.59), kind=kLoop, calls=%fused_computation | loop fusion | bytes 3072 | tf_op jit(solution)/shard_map/squeeze | solution.py:202

commit v4 on v3

--- a/solution.py
+++ b/solution.py
@@ -10,6 +10,7 @@
 EPS = 1e-6
 LANES = 128
 BLOCK = 512
+GROUP = 64
 CHUNK = 2 * BLOCK
 SLOTS = 7
 MESH = pl.DeviceIdType.MESH
@@ -78,17 +79,19 @@
                                preferred_element_type=jnp.float32)
 
     def fold(z_ref, first):
-        z = z_ref[...].reshape(BLOCK // 8, 8, width)
-        m_old = m_ref[...]
-        m_new = jnp.maximum(m_old, jnp.max(z, axis=0))
-        scale = jnp.exp(m_old - m_new)
-        e = jnp.exp(z - m_new[None])
-        m_ref[...] = m_new
-        s_ref[...] = s_ref[...] * scale + jnp.sum(e, axis=0)
-        a_ref[...] = a_ref[...] * scale + jnp.sum(e * z, axis=0)
-        here = wanted - first
-        at = 8 * lax.broadcasted_iota(jnp.int32, z.shape, 0)
-        p_ref[...] += jnp.sum(jnp.where(here[None] == at, z, 0.0), axis=0)
+        m, total, weighted, pick = m_ref[...], s_ref[...], a_ref[...], p_ref[...]
+        for group in range(BLOCK // GROUP):
+            z = z_ref[group * GROUP:(group + 1) * GROUP, :].reshape(GROUP // 8, 8, width)
+            m_new = jnp.maximum(m, jnp.max(z, axis=0))
+            scale = jnp.exp(m - m_new)
+            e = jnp.exp(z - m_new[None])
+            m = m_new
+            total = total * scale + jnp.sum(e, axis=0)
+            weighted = weighted * scale + jnp.sum(e * z, axis=0)
+            here = wanted - (first + group * GROUP)
+            for r in range(GROUP // 8):
+                pick = jnp.where(here == 8 * r, z[r], pick)
+        m_ref[...], s_ref[...], a_ref[...], p_ref[...] = m, total, weighted, pick
 
     e_copy(0, 0).wait()
     z_a[...] = logits(0, 0)

time: 64.5 us -> 64.1 us (level)
  no operation moved by 1% of the time
where the time goes in v4:
time: 64.1 us; the launch traced here: 63.7 us
  Pallas kernels  60.5 us (94%)
  local copies, waits for them, and re-layouts  2.62 us (4%)
    pallas_call x1, Pallas kernels, local_part(): pl.pallas_call(functools.partial(head_kernel, tp), out_shape=jax.ShapeDty...  60.5 us
    squeeze x1, local copies, waits for them, and re-layouts, local_part(): return (out[0], out[1])  1.32 us
    reshape x1, local copies, waits for them, and re-layouts, local_part(): norm_w.reshape(1, depth)  1.3 us

profile of v4, /device:TPU:0, one launch (start us, length us, event | category | flops | bytes accessed | tf_op | source)
XLA Modules:
  0.0 63.7 jit_solution(17810045811076144175)
XLA Ops:
  0.6 1.3 %reshape.7.w_ref = bf16[1,2560]{1,0:T(2,128)(2,1)} reshape(bf16[2560]{0:T(1024)(128)(2,1)} %param.5) | data formatting | bytes 10240 | tf_op jit(solution)/shard_map/reshape | solution.py:204
  1.9 60.5 %shard_map.59 = f32[2,16,12]{2,1,0:T(8,128)} custom-call(bf16[12,16,2560]{2,1,0:T(8,128)(2,1)} %bitcast.5, bf16[1,2560]{1,0:T(2,128)(2,1)} %reshape.7.w_ref, bf16[16384,2560]{1,0:T(8,128)(2,1)} %e_hbm.1, s32[16,12]{1,0:T(8,128)} %ids_ref.1), custom_call_target="tpu_custom_call" | custom-call | tf_op jit(solution)/shard_map/pallas_call | solution.py:179
  62.4 1.3 %slice_bitcast_fusion = (f32[16,12]{1,0:T(8,128)}, f32[16,12]{1,0:T(8,128)}) fusion(f32[2,16,12]{2,1,0:T(8,128)} %shard_map.59), kind=kLoop, calls=%fused_computation | loop fusion | bytes 3072 | tf_op jit(solution)/shard_map/squeeze | solution.py:205
